TPU v7x, 256 devices: a whole 4x4x8 slice. The times are simulated.
256 devices in a mesh: blk: 16 (over z, y_lo), grp: 16 (over x, y_hi, core).
Axes of the slice: x: 4, y: 4 (y_hi: 2, y_lo: 2; y = y_hi * 2 + y_lo), z: 8, core: 2. Of those that a mesh axis runs over, the one named last changes fastest.
Arguments:
- frames: bfloat16 [16, 4096, 1024], P('grp', 'blk'), may hold values from -16 to 16
- utt_lengths: int32 [8], replicated, may hold values from 1 to 16384, 65536 in all
- attn_gain: float32 [1024], replicated, may hold values from 0.25 to 1.75
- w_qkv: bfloat16 [1024, 3072], P(None, 'grp'), may hold values from -4 to 4
- w_out: bfloat16 [1024, 1024], replicated, may hold values from -0.375 to 0.375
- conv_gain: float32 [1024], replicated, may hold values from 0.25 to 1.75
- w_glu: bfloat16 [1024, 2048], replicated, may hold values from -0.1875 to 0.1875
- w_depth: float32 [31, 1024], replicated, may hold values from -1 to 1
- depth_gain: float32 [1024], replicated, may hold values from 0.25 to 1.75
- w_proj: bfloat16 [1024, 1024], replicated, may hold values from -0.1875 to 0.1875
Outputs:
- block_out: bfloat16 [16, 4096, 1024], P('grp', 'blk')
Inputs may be any that keep to these rules, and one draw needn't show every extreme that they name: `utt_lengths`: they sum to 65536 and the longest is exactly 16384.
All inputs are finite; a program needn't handle non-finite values.
Results may differ from a plain program's by a relative error of at most 0.0095.
Values may be sent and summed in bfloat16 or wider, within the bound.
No kernel may reach another device: no remote copies, remote signals or barrier semaphores. Data moves between devices by JAX's collectives and lax.ppermute only.
A program may use at most 192 MiB of HBM per device.

v0:
```python
import jax
import jax.numpy as jnp
from jax import lax
from jax.sharding import PartitionSpec as P

HEADS = 16
epsilon = 1e-05
big_negative = -1e30


def padded_2(block, sides, width, periodic):
    for axis, dim in sides:
        count = lax.axis_size(axis)
        forward = [(i, i + 1) for i in range(count - 1)]
        if periodic:
            forward.append((count - 1, 0))
        backward = [(target, source) for source, target in forward]
        low = lax.ppermute(
            lax.slice_in_dim(block, block.shape[dim] - width, None, axis=dim), axis, forward
        )
        high = lax.ppermute(lax.slice_in_dim(block, 0, width, axis=dim), axis, backward)
        block = jnp.concatenate([low, block, high], axis=dim)
    return block


def normalize(values, row_gain):
    center = values - jnp.mean(values, axis=-1, keepdims=True)
    spread = jnp.mean(center * center, axis=-1, keepdims=True)
    return center * lax.rsqrt(spread + epsilon) * row_gain


def segment_of(utt_lengths, positions):
    starts = jnp.cumsum(utt_lengths) - utt_lengths
    started = (starts[None, :] <= positions[:, None]).astype(jnp.int32)
    return jnp.sum(started, axis=1) - 1


def body(
    frames, utt_lengths, attn_gain, w_qkv, w_out, conv_gain, w_glu, w_depth, depth_gain, w_proj
):
    frame_rows = frames.shape[1]
    width = frames.shape[2]
    head_count = HEADS
    head_width = width // head_count
    kernel_half = (w_depth.shape[0] - 1) // 2
    score_scale = head_width ** (-0.5)
    blocks = lax.axis_size("blk")
    block_index = lax.axis_index("blk")
    group_index = lax.axis_index("grp")
    window = frame_rows * blocks
    window_start = group_index * window
    first_frame = window_start + block_index * frame_rows
    local_frames = frames[0]
    local_float = local_frames.astype(jnp.float32)
    normed = normalize(local_float, attn_gain).astype(jnp.bfloat16)
    qkv_rows = jnp.dot(
        normed, lax.all_gather(w_qkv, "grp", axis=1, tiled=True), preferred_element_type=jnp.float32
    ).astype(jnp.bfloat16)
    local_seg = segment_of(utt_lengths, first_frame + jnp.arange(frame_rows, dtype=jnp.int32))
    my_heads = lax.all_to_all(qkv_rows, "blk", split_axis=1, concat_axis=0, tiled=True)
    local_heads = head_count // blocks
    qkv_split = my_heads.reshape(window, local_heads, 3, head_width)
    query_all = qkv_split[:, :, 0, :]
    keys_all = qkv_split[:, :, 1, :]
    values_all = qkv_split[:, :, 2, :]
    window_seg = segment_of(utt_lengths, window_start + jnp.arange(window, dtype=jnp.int32))
    query_block = min(512, window)
    block_count = window // query_block

    def attend(block_id):
        block_start = block_id * query_block
        queries = lax.dynamic_slice_in_dim(query_all, block_start, query_block, 0)
        query_seg = lax.dynamic_slice_in_dim(window_seg, block_start, query_block, 0)
        allowed = (query_seg[:, None] == window_seg[None, :])[None]
        scores = (
            jnp.einsum("qhd,khd->hqk", queries, keys_all, preferred_element_type=jnp.float32)
            * score_scale
        )
        row_max = jnp.max(jnp.where(allowed, scores, big_negative), axis=2, keepdims=True)
        weights = jnp.where(allowed, jnp.exp(scores - row_max), 0.0)
        row_total = jnp.sum(weights, axis=2)
        mixed_values = jnp.einsum(
            "hqk,khd->qhd",
            weights.astype(jnp.bfloat16),
            values_all,
            preferred_element_type=jnp.float32,
        )
        normed_values = mixed_values / jnp.transpose(row_total)[:, :, None]
        return normed_values.reshape(query_block, local_heads * head_width).astype(jnp.bfloat16)

    pieces = lax.map(attend, jnp.arange(block_count, dtype=jnp.int32))
    merged_heads = pieces.reshape(window, local_heads * head_width)
    attended = lax.all_to_all(merged_heads, "blk", split_axis=0, concat_axis=1, tiled=True)
    residual = (local_float + jnp.dot(attended, w_out, preferred_element_type=jnp.float32)).astype(
        jnp.bfloat16
    )
    residual = lax.optimization_barrier(residual)
    conv_in = normalize(residual.astype(jnp.float32), conv_gain).astype(jnp.bfloat16)
    projected = jnp.dot(conv_in, w_glu, preferred_element_type=jnp.float32)
    gated = (projected[:, :width] * jax.nn.sigmoid(projected[:, width:])).astype(jnp.bfloat16)
    gated = lax.optimization_barrier(gated)
    padded = padded_2(gated, (("blk", 0),), kernel_half, True)
    left_rim = padded[:kernel_half]
    right_rim = padded[frame_rows + kernel_half :]
    outer_rims = padded_2(jnp.stack([right_rim, left_rim]), (("grp", 0),), 1, False)
    left_edge = jnp.where(block_index == 0, outer_rims[0], left_rim)
    right_edge = jnp.where(block_index == blocks - 1, outer_rims[3], right_rim)
    extended = jnp.concatenate([left_edge, gated, right_edge], axis=0).astype(jnp.float32)
    extended_seg = segment_of(
        utt_lengths,
        first_frame - kernel_half + jnp.arange(frame_rows + 2 * kernel_half, dtype=jnp.int32),
    )
    mixed_conv = jnp.zeros((frame_rows, width), jnp.float32)
    for offset in range(2 * kernel_half + 1):
        same_seg = (extended_seg[offset : offset + frame_rows] == local_seg)[:, None]
        mixed_conv = mixed_conv + jnp.where(
            same_seg, extended[offset : offset + frame_rows] * w_depth[offset], 0.0
        )
    normed_conv = normalize(mixed_conv, depth_gain)
    activated = (normed_conv * jax.nn.sigmoid(normed_conv)).astype(jnp.bfloat16)
    result = (
        residual.astype(jnp.float32)
        + jnp.dot(activated, w_proj, preferred_element_type=jnp.float32)
    ).astype(jnp.bfloat16)
    return result[None]


def solution(mesh):
    in_specs = (P("grp", "blk", None), P(), P(), P(None, "grp"), P(), P(), P(), P(), P(), P())
    out_specs = P("grp", "blk", None)
    return jax.shard_map(body, mesh=mesh, in_specs=in_specs, out_specs=out_specs, check_vma=False)
```

profile of v0, /device:TPU:1, one launch (start us, length us, event | category | flops | bytes accessed | tf_op | source)
XLA Modules:
  0.0 285.7 jit_solution(17601344647619971981)
XLA Ops:
  6.5 0.7 all-gather.2.cloned.1.call-update
  7.3 1.2 convert_reduce_fusion.1
  8.5 1.3 fusion.39
  9.8 73.4 %all-gather.2.cloned.1.call-done = bf16[1024,3072]{0,1:T(8,128)(2,1)} async-done(((bf16[1024,192]{0,1:T(8,128)(2,1)}), bf16[1024,3072]{0,1:T(8,128)(2,1)}) %all-gather.2.cloned.1.call-update) | async-done | bytes 6291472 | tf_op jit(solution)/shard_map/all_gather | solution.py:57
  83.2 6.0 %convolution_convert_fusion = bf16[256,3072]{1,0:T(8,128)(2,1)} fusion(bf16[1024,3072]{0,1:T(8,128)(2,1)} %all-gather.2.cloned.1.call-done, bf16[1,256,1024]{2,1,0:T(8,128)(2,1)} %param.12, f32[1024]{0:T(1024)} %param.14, f32[256]{0:T(256)S(1)} %add_rsqrt_fusion.2, f32[256]{0:T(256)S(1)} %broadcast_multiply_fusion.2), kind=kOutput, calls=%fused_computation.19 | convolution fusion | flops 1612709888 | bytes 8394752 | tf_op jit(solution)/shard_map/dot_general | solution.py:56
  89.2 2.6 copy.19
  91.8 6.9 %all-to-all-start = ((bf16[256,16,192]{0,2,1:T(8,128)(2,1)}), bf16[256,16,192]{0,2,1:T(8,128)(2,1)}, u32[]{:S(2)}, u32[]{:S(2)}) async-start(bf16[256,16,192]{0,2,1:T(8,128)(2,1)} %bitcast.125), calls=%async_computation | async-start | bytes 3145728 | tf_op jit(solution)/shard_map/all_to_all | solution.py:60
  98.7 0.2 reduce-window.9
  99.1 35.8 %all-to-all-done = bf16[256,16,192]{0,2,1:T(8,128)(2,1)} async-done(((bf16[256,16,192]{0,2,1:T(8,128)(2,1)}), bf16[256,16,192]{0,2,1:T(8,128)(2,1)}, u32[]{:S(2)}, u32[]{:S(2)}) %all-to-all-start) | async-done | bytes 1572896 | tf_op jit(solution)/shard_map/all_to_all | solution.py:60
  134.8 3.4 %copy.20 = bf16[16,256,192]{1,0,2:T(8,128)(2,1)} copy(bf16[16,256,192]{1,2,0:T(8,128)(2,1)} %bitcast.12) | data formatting | bytes 3145728 | tf_op jit(solution)/shard_map/all_to_all | solution.py:60
  138.3 3.8 %reshape.169 = bf16[4096,1,3,64]{0,3,2,1:T(8,128)(2,1)} reshape(bf16[16,256,192]{1,0,2:T(8,128)(2,1)} %copy.20) | data formatting | bytes 3145728 | tf_op jit(solution)/shard_map/reshape | solution.py:62
  142.0 2.5 slice_bitcast_fusion
  144.5 75.0 %while.10 = (s32[]{:T(128)}, bf16[8,512,64]{1,2,0:T(8,128)(2,1)}, s32[8]{0:T(128)S(1)}, s32[4096]{0:T(1024)S(1)}, bf16[4096,1,64]{0,2,1:T(8,128)(2,1)}, /*index=...) while((s32[]{:T(128)}, bf16[8,512,64]{1,2,0:T(8,128)(2,1)}, ...), condition=%wide.region_7.8_spmd, body=%wide.region_4.0_spmd.sunk | while | flops 566295552 | bytes 26415792 | solution.py:91
  144.5 0.6 dynamic_slice.20
  145.8 2.7 fusion.139
  148.5 2.5 fusion.140
  150.9 3.0 %fusion.141 = bf16[8,512,64]{1,2,0:T(8,128)(2,1)} fusion(bf16[8,512,64]{1,2,0:T(8,128)(2,1)} %get-tuple-element.187, s32[]{:T(128)} %get-tuple-element.186, f32[512,4096]{1,0:T(8,128)S(1)} %get-tuple-element.173, f32[512]{0:T(512)S(1)} %get-tuple-element.174, s32[4096]{0:T(1024)S(1)} %get-tuple-element.200, s32[512]{0:T(512)S(1)} %dynamic_slice.21, ...), kind=kOutput, calls=%fused_computation.10.clone.1 | convolution fusion | flops 278986752 | bytes 9001472 | tf_op jit(solution)/shard_map/while/body/eval_jaxpr/hqk,khd->qhd/dot_general | solution.py:82
  153.9 0.6 dynamic_slice.20
  155.2 2.6 fusion.139
  157.8 2.5 fusion.140
  160.3 3.0 %fusion.141 = bf16[8,512,64]{1,2,0:T(8,128)(2,1)} fusion(bf16[8,512,64]{1,2,0:T(8,128)(2,1)} %get-tuple-element.187, s32[]{:T(128)} %get-tuple-element.186, f32[512,4096]{1,0:T(8,128)S(1)} %get-tuple-element.173, f32[512]{0:T(512)S(1)} %get-tuple-element.174, s32[4096]{0:T(1024)S(1)} %get-tuple-element.200, s32[512]{0:T(512)S(1)} %dynamic_slice.21, ...), kind=kOutput, calls=%fused_computation.10.clone.1 | convolution fusion | flops 278986752 | bytes 9001472 | tf_op jit(solution)/shard_map/while/body/eval_jaxpr/hqk,khd->qhd/dot_general | solution.py:82
  163.3 0.6 dynamic_slice.20
  164.6 2.7 fusion.139
  167.2 2.5 fusion.140
  169.7 3.0 %fusion.141 = bf16[8,512,64]{1,2,0:T(8,128)(2,1)} fusion(bf16[8,512,64]{1,2,0:T(8,128)(2,1)} %get-tuple-element.187, s32[]{:T(128)} %get-tuple-element.186, f32[512,4096]{1,0:T(8,128)S(1)} %get-tuple-element.173, f32[512]{0:T(512)S(1)} %get-tuple-element.174, s32[4096]{0:T(1024)S(1)} %get-tuple-element.200, s32[512]{0:T(512)S(1)} %dynamic_slice.21, ...), kind=kOutput, calls=%fused_computation.10.clone.1 | convolution fusion | flops 278986752 | bytes 9001472 | tf_op jit(solution)/shard_map/while/body/eval_jaxpr/hqk,khd->qhd/dot_general | solution.py:82
  172.6 0.6 dynamic_slice.20
  173.9 2.6 fusion.139
  176.6 2.5 fusion.140
  179.1 3.0 %fusion.141 = bf16[8,512,64]{1,2,0:T(8,128)(2,1)} fusion(bf16[8,512,64]{1,2,0:T(8,128)(2,1)} %get-tuple-element.187, s32[]{:T(128)} %get-tuple-element.186, f32[512,4096]{1,0:T(8,128)S(1)} %get-tuple-element.173, f32[512]{0:T(512)S(1)} %get-tuple-element.174, s32[4096]{0:T(1024)S(1)} %get-tuple-element.200, s32[512]{0:T(512)S(1)} %dynamic_slice.21, ...), kind=kOutput, calls=%fused_computation.10.clone.1 | convolution fusion | flops 278986752 | bytes 9001472 | tf_op jit(solution)/shard_map/while/body/eval_jaxpr/hqk,khd->qhd/dot_general | solution.py:82
  182.0 0.6 dynamic_slice.20
  183.3 2.7 fusion.139
  186.0 2.5 fusion.140
  188.4 3.0 %fusion.141 = bf16[8,512,64]{1,2,0:T(8,128)(2,1)} fusion(bf16[8,512,64]{1,2,0:T(8,128)(2,1)} %get-tuple-element.187, s32[]{:T(128)} %get-tuple-element.186, f32[512,4096]{1,0:T(8,128)S(1)} %get-tuple-element.173, f32[512]{0:T(512)S(1)} %get-tuple-element.174, s32[4096]{0:T(1024)S(1)} %get-tuple-element.200, s32[512]{0:T(512)S(1)} %dynamic_slice.21, ...), kind=kOutput, calls=%fused_computation.10.clone.1 | convolution fusion | flops 278986752 | bytes 9001472 | tf_op jit(solution)/shard_map/while/body/eval_jaxpr/hqk,khd->qhd/dot_general | solution.py:82
  191.4 0.6 dynamic_slice.20
  192.7 2.6 fusion.139
  195.4 2.5 fusion.140
  197.8 3.0 %fusion.141 = bf16[8,512,64]{1,2,0:T(8,128)(2,1)} fusion(bf16[8,512,64]{1,2,0:T(8,128)(2,1)} %get-tuple-element.187, s32[]{:T(128)} %get-tuple-element.186, f32[512,4096]{1,0:T(8,128)S(1)} %get-tuple-element.173, f32[512]{0:T(512)S(1)} %get-tuple-element.174, s32[4096]{0:T(1024)S(1)} %get-tuple-element.200, s32[512]{0:T(512)S(1)} %dynamic_slice.21, ...), kind=kOutput, calls=%fused_computation.10.clone.1 | convolution fusion | flops 278986752 | bytes 9001472 | tf_op jit(solution)/shard_map/while/body/eval_jaxpr/hqk,khd->qhd/dot_general | solution.py:82
  200.8 0.6 dynamic_slice.20
  202.1 2.7 fusion.139
  204.7 2.5 fusion.140
  207.2 3.0 %fusion.141 = bf16[8,512,64]{1,2,0:T(8,128)(2,1)} fusion(bf16[8,512,64]{1,2,0:T(8,128)(2,1)} %get-tuple-element.187, s32[]{:T(128)} %get-tuple-element.186, f32[512,4096]{1,0:T(8,128)S(1)} %get-tuple-element.173, f32[512]{0:T(512)S(1)} %get-tuple-element.174, s32[4096]{0:T(1024)S(1)} %get-tuple-element.200, s32[512]{0:T(512)S(1)} %dynamic_slice.21, ...), kind=kOutput, calls=%fused_computation.10.clone.1 | convolution fusion | flops 278986752 | bytes 9001472 | tf_op jit(solution)/shard_map/while/body/eval_jaxpr/hqk,khd->qhd/dot_general | solution.py:82
  210.2 0.6 dynamic_slice.20
  211.5 2.6 fusion.139
  214.1 2.5 fusion.140
  216.6 3.0 %fusion.141 = bf16[8,512,64]{1,2,0:T(8,128)(2,1)} fusion(bf16[8,512,64]{1,2,0:T(8,128)(2,1)} %get-tuple-element.187, s32[]{:T(128)} %get-tuple-element.186, f32[512,4096]{1,0:T(8,128)S(1)} %get-tuple-element.173, f32[512]{0:T(512)S(1)} %get-tuple-element.174, s32[4096]{0:T(1024)S(1)} %get-tuple-element.200, s32[512]{0:T(512)S(1)} %dynamic_slice.21, ...), kind=kOutput, calls=%fused_computation.10.clone.1 | convolution fusion | flops 278986752 | bytes 9001472 | tf_op jit(solution)/shard_map/while/body/eval_jaxpr/hqk,khd->qhd/dot_general | solution.py:82
  219.6 1.4 copy.21
  221.0 1.0 all_to_all.29
  221.9 2.0 copy.22
  223.9 6.8 %all-to-all-start.1 = ((bf16[16,256,64]{1,2,0:T(8,128)(2,1)}), bf16[16,256,64]{1,2,0:T(8,128)(2,1)S(1)}, u32[]{:S(2)}, u32[]{:S(2)}) async-start(bf16[16,256,64]{1,2,0:T(8,128)(2,1)} %copy.22), calls=%async_computation.1 | async-start | bytes 1048576 | tf_op jit(solution)/shard_map/all_to_all | solution.py:93
  231.1 15.4 %all-to-all-done.1 = bf16[16,256,64]{1,2,0:T(8,128)(2,1)S(1)} async-done(((bf16[16,256,64]{1,2,0:T(8,128)(2,1)}), bf16[16,256,64]{1,2,0:T(8,128)(2,1)S(1)}, u32[]{:S(2)}, u32[]{:S(2)}) %all-to-all-start.1) | async-done | bytes 524320 | tf_op jit(solution)/shard_map/all_to_all | solution.py:93
  246.5 0.8 copy-done.2
  247.3 1.9 fusion.29
  249.4 0.3 fusion.36
  249.7 1.4 fusion.109
  251.1 0.3 fusion.107
  251.4 0.3 collective-permute-start
  251.8 3.6 %collective-permute-start.2 = (bf16[15,1024]{1,0:T(8,128)(2,1)S(1)}, bf16[15,1024]{1,0:T(8,128)(2,1)S(1)}, u32[]{:S(2)}, u32[]{:S(2)}) collective-permute-start(bf16[15,1024]{1,0:T(8,128)(2,1)S(1)} %get-tuple-element.65), channel_id=1, source_target_pairs={{16,0},{32,16},{48,32},{64,48},{80,64},{96,80},{112,96},{128,112},... | collective-permute-start | bytes 92168 | tf_op jit(solution)/shard_map/ppermute | solution.py:21
  255.4 1.1 collective-permute-done
  256.5 7.0 %collective-permute-start.1 = (bf16[1,15,1024]{2,1,0:T(8,128)(2,1)S(1)}, bf16[1,15,1024]{2,1,0:T(8,128)(2,1)S(1)}, u32[]{:S(2)}, u32[]{:S(2)}) collective-permute-start(bf16[1,15,1024]{2,1,0:T(8,128)(2,1)S(1)} %bitcast.127), channel_id=1, source_target_pairs={{0,1},{1,2},{2,3},{3,4},{4,5},{5,6},{6,7},{7,8},{8,9},{9,10},{10,1... | collective-permute-start | bytes 92168 | tf_op jit(solution)/shard_map/ppermute | solution.py:18
  263.7 1.9 collective-permute-start.3
  265.6 4.8 %collective-permute-done.3 = bf16[1,15,1024]{2,1,0:T(8,128)(2,1)S(1)} collective-permute-done((bf16[1,15,1024]{2,1,0:T(8,128)(2,1)S(1)}, bf16[1,15,1024]{2,1,0:T(8,128)(2,1)S(1)}, u32[]{:S(2)}, u32[]{:S(2)}) %collective-permute-start.3) | collective-permute-done | bytes 30752 | tf_op jit(solution)/shard_map/ppermute | solution.py:21
  270.6 6.3 %fusion.122 = (f32[256]{0:T(256)S(1)}, f32[256,1024]{1,0:T(8,128)S(1)}) fusion(f32[1024]{0:T(1024)S(1)} %bitcast.139, f32[286,1024]{1,0:T(8,128)S(1)} %maximum_convert_fusion, pred[256]{0:T(512)(128)(4,1)S(1)} %get-tuple-element.98, f32[1024]{0:T(1024)S(1)} %bitcast.140, pred[256]{0:T(512)(128)(4,1)S(1)} %get-tuple-element.99, f32[1024]{0:T(1024)S(1)} %bitcast.142, ...), kind=kLoop, calls=%fused_computation.205 | loop fusion | flops 24379136 | bytes 33690368 | tf_op jit(solution)/shard_map/reduce_sum | solution.py:27
  276.9 0.2 multiply_reduce_fusion
  277.1 1.7 fusion.35
  (54 shorter events, 1.6 us)
Async XLA Ops:
  6.5 240.7 %copy-start = (bf16[1024,1024]{1,0:T(8,128)(2,1)S(1)}, bf16[1024,1024]{1,0:T(8,128)(2,1)}, u32[]{:S(2)}) copy-start(bf16[1024,1024]{1,0:T(8,128)(2,1)} %param.16) | copy-start | bytes 6291460
  6.5 76.6 %all-gather.2.cloned.1.call-start = ((), (), s32[]{:S(2)}) async-start(), calls=%async_computation.2 | async-start | bytes 6684672 | tf_op jit(solution)/shard_map/all_gather | solution.py:57
  89.2 9.5 %copy-start.8 = (s32[8]{0:T(128)S(1)}, s32[8]{0:T(128)}, u32[]{:S(2)}) copy-start(s32[8]{0:T(128)} %param.13) | copy-start | bytes 100
  91.8 43.0 %all-to-all-start = ((bf16[256,16,192]{0,2,1:T(8,128)(2,1)}), bf16[256,16,192]{0,2,1:T(8,128)(2,1)}, u32[]{:S(2)}, u32[]{:S(2)}) async-start(bf16[256,16,192]{0,2,1:T(8,128)(2,1)} %bitcast.125), calls=%async_computation | async-start | bytes 3145728 | tf_op jit(solution)/shard_map/all_to_all | solution.py:60
  219.5 11.4 %copy-start.3 = (f32[31,1024]{1,0:T(8,128)S(1)}, f32[31,1024]{1,0:T(8,128)}, u32[]{:S(2)}) copy-start(f32[31,1024]{1,0:T(8,128)} %param.19) | copy-start | bytes 380932
  219.5 27.7 %copy-start.1 = (bf16[1,256,1024]{2,1,0:T(8,128)(2,1)S(1)}, bf16[1,256,1024]{2,1,0:T(8,128)(2,1)}, u32[]{:S(2)}) copy-start(bf16[1,256,1024]{2,1,0:T(8,128)(2,1)} %param.12) | copy-start | bytes 1572868
  221.0 28.7 %copy-start.6 = (f32[1024]{0:T(1024)S(1)}, f32[1024]{0:T(1024)}, u32[]{:S(2)}) copy-start(f32[1024]{0:T(1024)} %param.17) | copy-start | bytes 12292
  223.9 22.6 %all-to-all-start.1 = ((bf16[16,256,64]{1,2,0:T(8,128)(2,1)}), bf16[16,256,64]{1,2,0:T(8,128)(2,1)S(1)}, u32[]{:S(2)}, u32[]{:S(2)}) async-start(bf16[16,256,64]{1,2,0:T(8,128)(2,1)} %copy.22), calls=%async_computation.1 | async-start | bytes 1048576 | tf_op jit(solution)/shard_map/all_to_all | solution.py:93
  246.5 0.8 copy-start.2
  247.3 2.4 copy-start.4
  251.4 5.1 %collective-permute-start = (bf16[15,1024]{1,0:T(8,128)(2,1)S(1)}, bf16[15,1024]{1,0:T(8,128)(2,1)S(1)}, u32[]{:S(2)}, u32[]{:S(2)}) collective-permute-start(bf16[15,1024]{1,0:T(8,128)(2,1)S(1)} %get-tuple-element.64), channel_id=1, source_target_pairs={{0,16},{16,32},{32,48},{48,64},{64,80},{80,96},{96,112},{112,128},... | collective-permute-start | bytes 92168 | tf_op jit(solution)/shard_map/ppermute | solution.py:18
  251.8 11.8 %collective-permute-start.2 = (bf16[15,1024]{1,0:T(8,128)(2,1)S(1)}, bf16[15,1024]{1,0:T(8,128)(2,1)S(1)}, u32[]{:S(2)}, u32[]{:S(2)}) collective-permute-start(bf16[15,1024]{1,0:T(8,128)(2,1)S(1)} %get-tuple-element.65), channel_id=1, source_target_pairs={{16,0},{32,16},{48,32},{64,48},{80,64},{96,80},{112,96},{128,112},... | collective-permute-start | bytes 92168 | tf_op jit(solution)/shard_map/ppermute | solution.py:21
  256.5 9.1 %collective-permute-start.1 = (bf16[1,15,1024]{2,1,0:T(8,128)(2,1)S(1)}, bf16[1,15,1024]{2,1,0:T(8,128)(2,1)S(1)}, u32[]{:S(2)}, u32[]{:S(2)}) collective-permute-start(bf16[1,15,1024]{2,1,0:T(8,128)(2,1)S(1)} %bitcast.127), channel_id=1, source_target_pairs={{0,1},{1,2},{2,3},{3,4},{4,5},{5,6},{6,7},{7,8},{8,9},{9,10},{10,1... | collective-permute-start | bytes 92168 | tf_op jit(solution)/shard_map/ppermute | solution.py:18
  263.7 6.7 %collective-permute-start.3 = (bf16[1,15,1024]{2,1,0:T(8,128)(2,1)S(1)}, bf16[1,15,1024]{2,1,0:T(8,128)(2,1)S(1)}, u32[]{:S(2)}, u32[]{:S(2)}) collective-permute-start(bf16[1,15,1024]{2,1,0:T(8,128)(2,1)S(1)} %bitcast.128), channel_id=1, source_target_pairs={{1,0},{2,1},{3,2},{4,3},{5,4},{6,5},{7,6},{8,7},{9,8},{10,9},{11,1... | collective-permute-start | bytes 92168 | tf_op jit(solution)/shard_map/ppermute | solution.py:21
  270.6 6.6 %copy-start.5 = (bf16[1024,1024]{1,0:T(8,128)(2,1)S(1)}, bf16[1024,1024]{1,0:T(8,128)(2,1)}, u32[]{:S(2)}) copy-start(bf16[1024,1024]{1,0:T(8,128)(2,1)} %param.21) | copy-start | bytes 6291460
  270.6 6.6 %copy-start.7 = (f32[1024]{0:T(1024)S(1)}, f32[1024]{0:T(1024)}, u32[]{:S(2)}) copy-start(f32[1024]{0:T(1024)} %param.20) | copy-start | bytes 12292
Sparse Core Ops, SparseCore 0:
  10.0 73.0 all-gather.1
where the time goes:
time: 287 us; the launch traced here: 286 us
  waiting for transfers between devices  131 us (46%)
  matrix products  55.9 us (19%)
  other arithmetic  30.3 us (11%)
  starting transfers between devices  26.6 us (9%)
  local copies, waits for them, and re-layouts  22.9 us (8%)
  between operations  13.7 us (5%)
  loops' own time  5.04 us (2%)
    all_gather x1, waiting for transfers between devices, body(): lax.all_gather(w_qkv, 'grp', axis=1, tiled=True)  73.4 us
    all_to_all x1, waiting for transfers between devices, body(): lax.all_to_all(qkv_rows, 'blk', split_axis=1, concat_axis=0, tiled=True)  35.8 us
    dot_general x8, matrix products, attend(): jnp.einsum('hqk,khd->qhd', weights.astype(jnp.bfloat16), values_all, pref...  23.7 us
    dot_general x8, matrix products, attend(): jnp.einsum('qhd,khd->hqk', queries, keys_all, preferred_element_type=jnp....  21.2 us
    reduce_sum x8, other arithmetic, attend(): row_total = jnp.sum(weights, axis=2)  19.8 us
    all_to_all x1, waiting for transfers between devices, body(): lax.all_to_all(merged_heads, 'blk', split_axis=0, concat_axis=1, tiled=True)  15.4 us
    reduce_sum x3, other arithmetic, normalize(): center = values - jnp.mean(values, axis=-1, keepdims=True)  7.59 us
    ppermute x2, starting transfers between devices, padded_2(): lax.ppermute(lax.slice_in_dim(block, block.shape[dim] - width, None, axis...  7.35 us
  transfers between devices with their start and end apart: 7, of which 5 were waited for; matrix products, arithmetic and copies ran while one was open for 1% of the time, Pallas kernels for 0%

commit v1 on v0

--- a/solution.py
+++ b/solution.py
@@ -53,9 +53,16 @@
     local_frames = frames[0]
     local_float = local_frames.astype(jnp.float32)
     normed = normalize(local_float, attn_gain).astype(jnp.bfloat16)
-    qkv_rows = jnp.dot(
-        normed, lax.all_gather(w_qkv, "grp", axis=1, tiled=True), preferred_element_type=jnp.float32
-    ).astype(jnp.bfloat16)
+
+    def choose_the_array(vals):
+        x_next = lax.axis_size("grp")
+        opened = jnp.stack([vals] * x_next, 0)
+        raw_out = lax.all_to_all(opened, axis_name="grp", split_axis=0, concat_axis=0)
+        return jnp.concatenate(raw_out, 1)
+
+    qkv_rows = jnp.dot(normed, choose_the_array(w_qkv), preferred_element_type=jnp.float32).astype(
+        jnp.bfloat16
+    )
     local_seg = segment_of(utt_lengths, first_frame + jnp.arange(frame_rows, dtype=jnp.int32))
     my_heads = lax.all_to_all(qkv_rows, "blk", split_axis=1, concat_axis=0, tiled=True)
     local_heads = head_count // blocks

time: 287 us -> 307 us (1.070)
  the two profiles are of different devices: /device:TPU:1 before, /device:TPU:5 now
where the time goes in v1:
time: 307 us; the launch traced here: 306 us
  waiting for transfers between devices  140 us (46%)
  starting transfers between devices  52.5 us (17%)
  matrix products  50.8 us (17%)
  local copies, waits for them, and re-layouts  28.4 us (9%)
  other arithmetic  28.3 us (9%)
  loops' own time  5.32 us (2%)
    all_to_all x1, waiting for transfers between devices, choose_the_array(): lax.all_to_all(opened, axis_name='grp', split_axis=0, concat_axis=0)  83.3 us
    all_to_all x1, waiting for transfers between devices, body(): lax.all_to_all(qkv_rows, 'blk', split_axis=1, concat_axis=0, tiled=True)  35.7 us
    ppermute x2, starting transfers between devices, padded_2(): lax.ppermute(lax.slice_in_dim(block, block.shape[dim] - width, None, axis...  23.8 us
    dot_general x8, matrix products, attend(): jnp.einsum('qhd,khd->hqk', queries, keys_all, preferred_element_type=jnp....  21.2 us
    reduce_sum x8, other arithmetic, attend(): row_total = jnp.sum(weights, axis=2)  19.8 us
    dot_general x8, matrix products, attend(): jnp.einsum('hqk,khd->qhd', weights.astype(jnp.bfloat16), values_all, pref...  18.8 us
    all_to_all x1, waiting for transfers between devices, body(): lax.all_to_all(merged_heads, 'blk', split_axis=0, concat_axis=1, tiled=True)  15.5 us
    all_to_all x1, starting transfers between devices, body(): lax.all_to_all(qkv_rows, 'blk', split_axis=1, concat_axis=0, tiled=True)  8.45 us
  transfers between devices with their start and end apart: 7, of which 5 were waited for; matrix products, arithmetic and copies ran while one was open for 0% of the time, Pallas kernels for 0%

profile of v1, /device:TPU:5, one launch (start us, length us, event | category | flops | bytes accessed | tf_op | source)
XLA Modules:
  0.0 306.1 jit_solution(15594959586024860666)
XLA Ops:
  0.0 4.6 %stack.6 = bf16[16,1024,192]{1,2,0:T(8,128)(2,1)} broadcast(bf16[1024,192]{0,1:T(8,128)(2,1)} %param.15), dimensions={1,2} | broadcast | bytes 6684672 | tf_op jit(solution)/shard_map/stack | solution.py:59
  4.6 7.9 %all-to-all-start = ((bf16[16,1024,192]{1,2,0:T(8,128)(2,1)}), bf16[16,1024,192]{1,2,0:T(8,128)(2,1)}, u32[]{:S(2)}, u32[]{:S(2)}) async-start(bf16[16,1024,192]{1,2,0:T(8,128)(2,1)} %stack.6), calls=%async_computation | async-start | bytes 12582912 | tf_op jit(solution)/shard_map/all_to_all | solution.py:60
  12.6 0.3 fusion.38
  12.9 83.3 %all-to-all-done = bf16[16,1024,192]{1,2,0:T(8,128)(2,1)} async-done(((bf16[16,1024,192]{1,2,0:T(8,128)(2,1)}), bf16[16,1024,192]{1,2,0:T(8,128)(2,1)}, u32[]{:S(2)}, u32[]{:S(2)}) %all-to-all-start) | async-done | bytes 6291488 | tf_op jit(solution)/shard_map/all_to_all | solution.py:60
  96.3 5.8 %convolution_convert_fusion = bf16[256,3072]{1,0:T(8,128)(2,1)} fusion(bf16[1024,3072]{0,1:T(8,128)(2,1)} %bitcast.13, bf16[1,256,1024]{2,1,0:T(8,128)(2,1)S(1)} %copy-done.1, f32[1024]{0:T(1024)S(1)} %copy-done.8, f32[256]{0:T(256)S(1)} %add_rsqrt_fusion.2, f32[256]{0:T(256)S(1)} %broadcast_multiply_fusion.2), kind=kOutput, calls=%fused_computation.19 | convolution fusion | flops 1612709888 | bytes 8394752 | tf_op jit(solution)/shard_map/dot_general | solution.py:63
  102.1 2.6 copy.20
  104.7 8.4 %all-to-all-start.1 = ((bf16[256,16,192]{0,2,1:T(8,128)(2,1)}), bf16[256,16,192]{0,2,1:T(8,128)(2,1)}, u32[]{:S(2)}, u32[]{:S(2)}) async-start(bf16[256,16,192]{0,2,1:T(8,128)(2,1)} %bitcast.124), calls=%async_computation.1 | async-start | bytes 3145728 | tf_op jit(solution)/shard_map/all_to_all | solution.py:67
  113.2 0.2 reduce-window.9
  113.5 35.7 %all-to-all-done.1 = bf16[256,16,192]{0,2,1:T(8,128)(2,1)} async-done(((bf16[256,16,192]{0,2,1:T(8,128)(2,1)}), bf16[256,16,192]{0,2,1:T(8,128)(2,1)}, u32[]{:S(2)}, u32[]{:S(2)}) %all-to-all-start.1) | async-done | bytes 1572896 | tf_op jit(solution)/shard_map/all_to_all | solution.py:67
  149.2 3.4 %copy.21 = bf16[16,256,192]{1,0,2:T(8,128)(2,1)} copy(bf16[16,256,192]{1,2,0:T(8,128)(2,1)} %bitcast.15) | data formatting | bytes 3145728 | tf_op jit(solution)/shard_map/all_to_all | solution.py:67
  152.6 3.8 %reshape.200 = bf16[4096,1,3,64]{0,3,2,1:T(8,128)(2,1)} reshape(bf16[16,256,192]{1,0,2:T(8,128)(2,1)} %copy.21) | data formatting | bytes 3145728 | tf_op jit(solution)/shard_map/reshape | solution.py:69
  156.4 2.5 slice_bitcast_fusion
  158.9 70.5 %while.10 = (s32[]{:T(128)}, bf16[8,512,64]{1,2,0:T(8,128)(2,1)S(1)}, s32[8]{0:T(128)S(1)}, s32[4096]{0:T(1024)S(1)}, bf16[4096,1,64]{0,2,1:T(8,128)(2,1)}, /*in...) while((s32[]{:T(128)}, ...), condition=%wide.region_7.8_spmd, body=%wide.region_4.0_spmd.sunk | while | flops 566295552 | bytes 28512464 | solution.py:98
  158.9 0.6 dynamic_slice.20
  160.2 2.6 fusion.140
  162.9 2.5 fusion.141
  165.4 2.3 fusion.142
  167.7 0.6 dynamic_slice.20
  169.0 2.7 fusion.140
  171.7 2.5 fusion.141
  174.2 2.3 fusion.142
  176.6 0.6 dynamic_slice.20
  177.9 2.7 fusion.140
  180.5 2.5 fusion.141
  183.0 2.3 fusion.142
  185.4 0.6 dynamic_slice.20
  186.7 2.7 fusion.140
  189.3 2.5 fusion.141
  191.8 2.3 fusion.142
  194.2 0.6 dynamic_slice.20
  195.5 2.7 fusion.140
  198.2 2.5 fusion.141
  200.6 2.3 fusion.142
  203.0 0.6 dynamic_slice.20
  204.3 2.7 fusion.140
  207.0 2.5 fusion.141
  209.5 2.3 fusion.142
  211.8 0.6 dynamic_slice.20
  213.1 2.7 fusion.140
  215.8 2.5 fusion.141
  218.3 2.3 fusion.142
  220.6 0.6 dynamic_slice.20
  221.9 2.7 fusion.140
  224.6 2.5 fusion.141
  227.1 2.3 fusion.142
  229.5 0.8 copy-done.3
  230.3 1.4 copy.22
  231.6 1.0 all_to_all.33
  232.6 2.0 copy.23
  234.6 6.9 %all-to-all-start.2 = ((bf16[16,256,64]{1,2,0:T(8,128)(2,1)}), bf16[16,256,64]{1,2,0:T(8,128)(2,1)S(1)}, u32[]{:S(2)}, u32[]{:S(2)}) async-start(bf16[16,256,64]{1,2,0:T(8,128)(2,1)} %copy.23), calls=%async_computation.2 | async-start | bytes 1048576 | tf_op jit(solution)/shard_map/all_to_all | solution.py:100
  241.8 15.5 %all-to-all-done.2 = bf16[16,256,64]{1,2,0:T(8,128)(2,1)S(1)} async-done(((bf16[16,256,64]{1,2,0:T(8,128)(2,1)}), bf16[16,256,64]{1,2,0:T(8,128)(2,1)S(1)}, u32[]{:S(2)}, u32[]{:S(2)}) %all-to-all-start.2) | async-done | bytes 524320 | tf_op jit(solution)/shard_map/all_to_all | solution.py:100
  257.3 0.8 copy-done.2
  258.1 1.9 fusion.29
  260.2 0.3 fusion.34
  260.5 1.4 fusion.110
  261.9 0.3 fusion.107
  262.4 3.6 %collective-permute-start.2 = (bf16[15,1024]{1,0:T(8,128)(2,1)S(1)}, bf16[15,1024]{1,0:T(8,128)(2,1)S(1)}, u32[]{:S(2)}, u32[]{:S(2)}) collective-permute-start(bf16[15,1024]{1,0:T(8,128)(2,1)S(1)} %get-tuple-element.65), channel_id=1, source_target_pairs={{16,0},{32,16},{48,32},{64,48},{80,64},{96,80},{112,96},{128,112},... | collective-permute-start | bytes 92168 | tf_op jit(solution)/shard_map/ppermute | solution.py:21
  266.0 1.1 collective-permute-done
  267.2 23.6 %collective-permute-start.1 = (bf16[1,15,1024]{2,1,0:T(8,128)(2,1)S(1)}, bf16[1,15,1024]{2,1,0:T(8,128)(2,1)S(1)}, u32[]{:S(2)}, u32[]{:S(2)}) collective-permute-start(bf16[1,15,1024]{2,1,0:T(8,128)(2,1)S(1)} %bitcast.126), channel_id=1, source_target_pairs={{0,1},{1,2},{2,3},{3,4},{4,5},{5,6},{6,7},{7,8},{8,9},{9,10},{10,1... | collective-permute-start | bytes 92168 | tf_op jit(solution)/shard_map/ppermute | solution.py:18
  290.9 1.9 collective-permute-start.3
  292.9 4.8 %collective-permute-done.3 = bf16[1,15,1024]{2,1,0:T(8,128)(2,1)S(1)} collective-permute-done((bf16[1,15,1024]{2,1,0:T(8,128)(2,1)S(1)}, bf16[1,15,1024]{2,1,0:T(8,128)(2,1)S(1)}, u32[]{:S(2)}, u32[]{:S(2)}) %collective-permute-start.3) | collective-permute-done | bytes 30752 | tf_op jit(solution)/shard_map/ppermute | solution.py:21
  297.8 6.3 %fusion.123 = (f32[256]{0:T(256)S(1)}, f32[256,1024]{1,0:T(8,128)S(1)}) fusion(f32[1024]{0:T(1024)S(1)} %bitcast.138, f32[286,1024]{1,0:T(8,128)S(1)} %maximum_convert_fusion, pred[256]{0:T(512)(128)(4,1)S(1)} %get-tuple-element.98, f32[1024]{0:T(1024)S(1)} %bitcast.139, pred[256]{0:T(512)(128)(4,1)S(1)} %get-tuple-element.99, f32[1024]{0:T(1024)S(1)} %bitcast.141, ...), kind=kLoop, calls=%fused_computation.207 | loop fusion | flops 24379136 | bytes 33690368 | tf_op jit(solution)/shard_map/reduce_sum | solution.py:27
  304.2 0.2 multiply_reduce_fusion
  304.4 1.7 fusion.33
  (74 shorter events, 1.9 us)
Async XLA Ops:
  0.0 258.1 %copy-start = (bf16[1024,1024]{1,0:T(8,128)(2,1)S(1)}, bf16[1024,1024]{1,0:T(8,128)(2,1)}, u32[]{:S(2)}) copy-start(bf16[1024,1024]{1,0:T(8,128)(2,1)} %param.16) | copy-start | bytes 6291460
  4.6 7.9 %copy-start.1 = (bf16[1,256,1024]{2,1,0:T(8,128)(2,1)S(1)}, bf16[1,256,1024]{2,1,0:T(8,128)(2,1)}, u32[]{:S(2)}) copy-start(bf16[1,256,1024]{2,1,0:T(8,128)(2,1)} %param.12) | copy-start | bytes 1572868
  4.6 91.7 %copy-start.8 = (f32[1024]{0:T(1024)S(1)}, f32[1024]{0:T(1024)}, u32[]{:S(2)}) copy-start(f32[1024]{0:T(1024)} %param.14) | copy-start | bytes 12292
  4.6 91.7 %all-to-all-start = ((bf16[16,1024,192]{1,2,0:T(8,128)(2,1)}), bf16[16,1024,192]{1,2,0:T(8,128)(2,1)}, u32[]{:S(2)}, u32[]{:S(2)}) async-start(bf16[16,1024,192]{1,2,0:T(8,128)(2,1)} %stack.6), calls=%async_computation | async-start | bytes 12582912 | tf_op jit(solution)/shard_map/all_to_all | solution.py:60
  102.1 11.1 %copy-start.11 = (s32[8]{0:T(128)S(1)}, s32[8]{0:T(128)}, u32[]{:S(2)}) copy-start(s32[8]{0:T(128)} %param.13) | copy-start | bytes 100
  104.7 44.5 %all-to-all-start.1 = ((bf16[256,16,192]{0,2,1:T(8,128)(2,1)}), bf16[256,16,192]{0,2,1:T(8,128)(2,1)}, u32[]{:S(2)}, u32[]{:S(2)}) async-start(bf16[256,16,192]{0,2,1:T(8,128)(2,1)} %bitcast.124), calls=%async_computation.1 | async-start | bytes 3145728 | tf_op jit(solution)/shard_map/all_to_all | solution.py:67
  162.9 2.5 copy-start.4
  171.7 2.5 copy-start.4
  180.5 2.5 copy-start.4
  189.3 2.5 copy-start.4
  198.1 2.5 copy-start.4
  207.0 2.5 copy-start.4
  215.8 2.5 copy-start.4
  224.6 2.5 copy-start.4
  229.5 0.8 copy-start.3
  230.2 11.5 %copy-start.5 = (f32[31,1024]{1,0:T(8,128)S(1)}, f32[31,1024]{1,0:T(8,128)}, u32[]{:S(2)}) copy-start(f32[31,1024]{1,0:T(8,128)} %param.19) | copy-start | bytes 380932
  231.6 28.9 %copy-start.9 = (f32[1024]{0:T(1024)S(1)}, f32[1024]{0:T(1024)}, u32[]{:S(2)}) copy-start(f32[1024]{0:T(1024)} %param.17) | copy-start | bytes 12292
  234.6 22.7 %all-to-all-start.2 = ((bf16[16,256,64]{1,2,0:T(8,128)(2,1)}), bf16[16,256,64]{1,2,0:T(8,128)(2,1)S(1)}, u32[]{:S(2)}, u32[]{:S(2)}) async-start(bf16[16,256,64]{1,2,0:T(8,128)(2,1)} %copy.23), calls=%async_computation.2 | async-start | bytes 1048576 | tf_op jit(solution)/shard_map/all_to_all | solution.py:100
  257.3 0.8 copy-start.2
  258.1 2.4 copy-start.6
  262.2 5.0 %collective-permute-start = (bf16[15,1024]{1,0:T(8,128)(2,1)S(1)}, bf16[15,1024]{1,0:T(8,128)(2,1)S(1)}, u32[]{:S(2)}, u32[]{:S(2)}) collective-permute-start(bf16[15,1024]{1,0:T(8,128)(2,1)S(1)} %get-tuple-element.64), channel_id=1, source_target_pairs={{0,16},{16,32},{32,48},{48,64},{64,80},{80,96},{96,112},{112,128},... | collective-permute-start | bytes 92168 | tf_op jit(solution)/shard_map/ppermute | solution.py:18
  262.4 28.5 %collective-permute-start.2 = (bf16[15,1024]{1,0:T(8,128)(2,1)S(1)}, bf16[15,1024]{1,0:T(8,128)(2,1)S(1)}, u32[]{:S(2)}, u32[]{:S(2)}) collective-permute-start(bf16[15,1024]{1,0:T(8,128)(2,1)S(1)} %get-tuple-element.65), channel_id=1, source_target_pairs={{16,0},{32,16},{48,32},{64,48},{80,64},{96,80},{112,96},{128,112},... | collective-permute-start | bytes 92168 | tf_op jit(solution)/shard_map/ppermute | solution.py:21
  267.2 25.7 %collective-permute-start.1 = (bf16[1,15,1024]{2,1,0:T(8,128)(2,1)S(1)}, bf16[1,15,1024]{2,1,0:T(8,128)(2,1)S(1)}, u32[]{:S(2)}, u32[]{:S(2)}) collective-permute-start(bf16[1,15,1024]{2,1,0:T(8,128)(2,1)S(1)} %bitcast.126), channel_id=1, source_target_pairs={{0,1},{1,2},{2,3},{3,4},{4,5},{5,6},{6,7},{7,8},{8,9},{9,10},{10,1... | collective-permute-start | bytes 92168 | tf_op jit(solution)/shard_map/ppermute | solution.py:18
  290.9 6.7 %collective-permute-start.3 = (bf16[1,15,1024]{2,1,0:T(8,128)(2,1)S(1)}, bf16[1,15,1024]{2,1,0:T(8,128)(2,1)S(1)}, u32[]{:S(2)}, u32[]{:S(2)}) collective-permute-start(bf16[1,15,1024]{2,1,0:T(8,128)(2,1)S(1)} %bitcast.127), channel_id=1, source_target_pairs={{1,0},{2,1},{3,2},{4,3},{5,4},{6,5},{7,6},{8,7},{9,8},{10,9},{11,1... | collective-permute-start | bytes 92168 | tf_op jit(solution)/shard_map/ppermute | solution.py:21
  297.8 6.6 %copy-start.7 = (bf16[1024,1024]{1,0:T(8,128)(2,1)S(1)}, bf16[1024,1024]{1,0:T(8,128)(2,1)}, u32[]{:S(2)}) copy-start(bf16[1024,1024]{1,0:T(8,128)(2,1)} %param.21) | copy-start | bytes 6291460
  297.8 6.6 %copy-start.10 = (f32[1024]{0:T(1024)S(1)}, f32[1024]{0:T(1024)}, u32[]{:S(2)}) copy-start(f32[1024]{0:T(1024)} %param.20) | copy-start | bytes 12292
